TPU v7x, 64 devices: a 2x2x8 block of a 4x4x8 slice. The times are simulated.
64 devices in a mesh: dp: 4 (over x, y), sp: 16 (over z, core).
Axes of the slice: x: 2, y: 2, z: 8, core: 2. Of those that a mesh axis runs over, the one named last changes fastest.
The devices are a block of a 4x4x8 slice.
Arguments:
- x_steps: bfloat16 [4, 64, 2560], P(None, 'dp'), parts along dimension 1
- k_cache: bfloat16 [64, 2048, 8, 128], P('dp', 'sp'), parts along dimension 0
- v_cache: bfloat16 [64, 2048, 8, 128], P('dp', 'sp'), parts along dimension 0
- seq_lens: int32 [64], P('dp'), parts along dimension 0
- norm_gain: bfloat16 [2560], replicated
- w_q: bfloat16 [2560, 4096], replicated
- w_k: bfloat16 [2560, 1024], replicated
- w_v: bfloat16 [2560, 1024], replicated
- w_o: bfloat16 [4096, 2560], replicated
- q_gain: bfloat16 [128], replicated
- k_gain: bfloat16 [128], replicated
Outputs:
- output 1: bfloat16 [4, 64, 2560], P(None, 'dp'), parts along dimension 1
- output 2: bfloat16 [64, 2048, 8, 128], P('dp', 'sp'), parts along dimension 0
- output 3: bfloat16 [64, 2048, 8, 128], P('dp', 'sp'), parts along dimension 0
There are 4 independent parts. A program takes and returns all parts, laid end to end along the dimension named above; an argument that names none is the same for every part.
All inputs are finite; a program needn't handle non-finite values.
Results may differ from a plain program's by a relative error of at most 0.0108835.
Values sent between devices are 32-bit elements.
A program may use at most 768 MiB of HBM per device.

v0:
```python
import math
import jax
import jax.numpy as jnp
from jax import lax
from jax.sharding import PartitionSpec as P

NORM_EPS = 1e-6
ROPE_BASE = 1000000.0


def rms_scale(values, gain):
    inv_rms = lax.rsqrt(jnp.mean(values * values, axis=-1, keepdims=True) + NORM_EPS)
    return values * inv_rms * gain.astype(jnp.float32)


def rope_rotate(values, positions):
    half_dim = values.shape[-1] // 2
    inv_freq = jnp.exp(jnp.arange(half_dim, dtype=jnp.float32) * (-2.0 * math.log(ROPE_BASE) / values.shape[-1]))
    angles = positions.astype(jnp.float32)[..., None, None] * inv_freq
    cosine = jnp.cos(angles)
    sine = jnp.sin(angles)
    lower_half = values[..., :half_dim]
    upper_half = values[..., half_dim:]
    return jnp.concatenate([lower_half * cosine - upper_half * sine, upper_half * cosine + lower_half * sine], axis=-1)


def project_steps(x_steps, positions, norm_gain, w_q, w_k, w_v, q_gain, k_gain):
    steps = x_steps.shape[0]
    batch = x_steps.shape[1]
    head_dim = q_gain.shape[0]
    normed = rms_scale(x_steps.astype(jnp.float32), norm_gain).astype(jnp.bfloat16)

    def heads_of(weight):
        flat_out = jnp.dot(normed, weight, preferred_element_type=jnp.float32).astype(jnp.bfloat16)
        return flat_out.reshape(steps, batch, -1, head_dim)

    queries = rope_rotate(rms_scale(heads_of(w_q).astype(jnp.float32), q_gain), positions).astype(jnp.bfloat16)
    keys_new = rope_rotate(rms_scale(heads_of(w_k).astype(jnp.float32), k_gain), positions).astype(jnp.bfloat16)
    return queries, keys_new, heads_of(w_v)


def local_partial(query, k_local, v_local, positions, first_slot):
    batch, slots, kv_heads, head_dim = k_local.shape
    grouped = query.reshape(batch, kv_heads, -1, head_dim)
    scores = jnp.einsum('bkgd,bskd->bkgs', grouped, k_local, preferred_element_type=jnp.float32) * head_dim ** -0.5
    slot_ids = first_slot + jnp.arange(slots)
    visible = slot_ids[None, :] <= positions[:, None]
    scores = jnp.where(visible[:, None, None, :], scores, -jnp.inf)
    row_max = jnp.maximum(jnp.max(scores, axis=-1), -1e30)
    weights = jnp.exp(scores - row_max[..., None])
    row_sum = jnp.sum(weights, axis=-1)
    part_out = jnp.einsum('bkgs,bskd->bkgd', weights.astype(jnp.bfloat16), v_local, preferred_element_type=jnp.float32)
    return part_out, row_max, row_sum


def solution(mesh):
    def per_device(x_steps, k_local, v_local, seq_lens, norm_gain, w_q, w_k, w_v, w_o, q_gain, k_gain):
        steps = x_steps.shape[0]
        batch, slots = k_local.shape[0], k_local.shape[1]
        positions = seq_lens[None, :] + jnp.arange(steps, dtype=jnp.int32)[:, None]
        queries, keys_new, vals_new = project_steps(x_steps, positions, norm_gain, w_q, w_k, w_v, q_gain, k_gain)
        first_slot = lax.axis_index('sp') * slots
        rows = jnp.arange(batch)
        attended_steps = []
        for step in range(steps):
            rel_pos = positions[step] - first_slot
            owned = (rel_pos >= 0) & (rel_pos < slots)
            write_pos = jnp.where(owned, rel_pos, slots)
            k_local = k_local.at[rows, write_pos].set(keys_new[step], mode='drop')
            v_local = v_local.at[rows, write_pos].set(vals_new[step], mode='drop')
            part_out, row_max, row_sum = local_partial(queries[step], k_local, v_local, positions[step], first_slot)
            glob_max = lax.pmax(row_max, 'sp')
            factor = jnp.exp(row_max - glob_max)
            numerator, denominator = lax.psum((part_out * factor[..., None], row_sum * factor), 'sp')
            attended_steps.append((numerator / denominator[..., None]).astype(jnp.bfloat16).reshape(batch, -1))
        attended = jnp.stack(attended_steps)
        out_proj = jnp.dot(attended, w_o, preferred_element_type=jnp.float32)
        y_steps = (x_steps.astype(jnp.float32) + out_proj).astype(jnp.bfloat16)
        return y_steps, k_local, v_local

    cache_spec = P('dp', 'sp', None, None)
    step_spec = P(None, 'dp', None)
    return jax.shard_map(per_device, mesh=mesh, in_specs=(step_spec, cache_spec, cache_spec, P('dp'), P(), P(), P(), P(), P(), P(), P()), out_specs=(step_spec, cache_spec, cache_spec), check_vma=False)
```

profile of v0, /device:TPU:21, one launch (start us, length us, event | category | flops | bytes accessed | tf_op | source)
XLA Modules:
  0.0 269.0 jit_solution(5922791192762145600)
XLA Ops:
  7.3 4.8 %copy.99 = bf16[16,128,8,128]{3,2,1,0:T(8,128)(2,1)} copy(bf16[16,128,8,128]{3,2,1,0:T(8,128)(2,1)} %param.13) | data formatting | bytes 8388608
  12.0 2.0 copy.98
  14.3 3.7 %fusion.78 = bf16[4,16,1024]{2,1,0:T(8,128)(2,1)S(1)} fusion(bf16[2560,1024]{1,0:T(8,128)(2,1)} %param.18, bf16[4,16,2560]{2,1,0:T(8,128)(2,1)S(1)} %copy-done, f32[2560]{0:T(1024)S(1)} %convert_element_type.75, f32[4,16]{1,0:T(4,128)S(1)} %add_rsqrt_fusion.2), kind=kOutput, calls=%fused_computation.50 | convolution fusion | flops 336265216 | bytes 5712128 | tf_op jit(solution)/shard_map/dot_general | solution.py:34
  18.1 9.1 %fusion.11 = f32[4,16,4096]{2,1,0:T(8,128)S(1)} fusion(bf16[2560,4096]{1,0:T(8,128)(2,1)} %param.16, bf16[4,16,2560]{2,1,0:T(8,128)(2,1)S(1)} %copy-done, f32[2560]{0:T(1024)S(1)} %convert_element_type.75, f32[4,16]{1,0:T(4,128)S(1)} %add_rsqrt_fusion.2), kind=kOutput, calls=%fused_computation.17 | convolution fusion | flops 1343356928 | bytes 22358272 | tf_op jit(solution)/shard_map/dot_general | solution.py:34
  27.8 1.1 fusion.75
  29.7 0.5 subtract_convert_fusion
  30.9 2.0 scatter_fusion
  33.0 4.5 %fusion.142 = (f32[16,8,4]{2,1,0:T(8,128)S(1)}, f32[16,8,4,128]{3,2,1,0:T(4,128)S(1)}) fusion(bf16[16,8,4,128]{3,2,1,0:T(4,128)(2,1)S(1)} %bitcast.125, bf16[16,128,8,128]{3,2,1,0:T(8,128)(2,1)} %scatter_fusion, pred[16,128]{1,0:T(8,128)(4,1)S(1)} %get-tuple-element.49), kind=kOutput, calls=%fused_computation.183 | convolution fusion | flops 16973312 | bytes 4591616 | tf_op jit(solution)/shard_map/bkgd,bskd->bkgs/dot_general | solution.py:45
  37.6 2.0 scatter_fusion.2
  39.6 4.5 %fusion.141 = (f32[16,8,4]{2,1,0:T(8,128)S(1)}, f32[16,8,4,128]{3,2,1,0:T(4,128)S(1)}) fusion(bf16[16,8,4,128]{3,2,1,0:T(4,128)(2,1)S(1)} %bitcast.124, bf16[16,128,8,128]{3,2,1,0:T(8,128)(2,1)} %scatter_fusion.2, pred[16,128]{1,0:T(8,128)(4,1)S(1)} %get-tuple-element.50), kind=kOutput, calls=%fused_computation.182 | convolution fusion | flops 16973312 | bytes 4591616 | tf_op jit(solution)/shard_map/bkgd,bskd->bkgs/dot_general | solution.py:45
  44.1 2.0 scatter_fusion.4
  46.2 4.5 %fusion.140 = (f32[16,8,4]{2,1,0:T(8,128)S(1)}, f32[16,8,4,128]{3,2,1,0:T(4,128)S(1)}) fusion(bf16[16,8,4,128]{3,2,1,0:T(4,128)(2,1)S(1)} %bitcast.123, bf16[16,128,8,128]{3,2,1,0:T(8,128)(2,1)} %scatter_fusion.4, pred[16,128]{1,0:T(8,128)(4,1)S(1)} %get-tuple-element.51), kind=kOutput, calls=%fused_computation.181 | convolution fusion | flops 16973312 | bytes 4591616 | tf_op jit(solution)/shard_map/bkgd,bskd->bkgs/dot_general | solution.py:45
  50.7 2.2 scatter_fusion.6
  52.9 4.5 %fusion.139 = (f32[16,8,4]{2,1,0:T(8,128)S(1)}, f32[16,8,4,128]{3,2,1,0:T(4,128)S(1)}) fusion(bf16[16,8,4,128]{3,2,1,0:T(4,128)(2,1)S(1)} %bitcast.122, bf16[16,128,8,128]{3,2,1,0:T(8,128)(2,1)} %scatter_fusion.6, pred[16,128]{1,0:T(8,128)(4,1)S(1)} %get-tuple-element.52), kind=kOutput, calls=%fused_computation.180 | convolution fusion | flops 16973312 | bytes 4591616 | tf_op jit(solution)/shard_map/bkgd,bskd->bkgs/dot_general | solution.py:45
  57.5 0.4 fusion.95
  58.3 54.2 %all-reduce.2 = (f32[16,8,4]{2,1,0:T(8,128)S(1)}, f32[16,8,4]{2,1,0:T(8,128)S(1)}, f32[16,8,4]{2,1,0:T(8,128)S(1)}, f32[16,8,4]{2,1,0:T(8,128)S(1)}) all-reduce(f32[16,8,4]{2,1,0:T(8,128)S(1)} %broadcast_maximum_fusion, f32[16,8,4]{2,1,0:T(8,128)S(1)} %broadcast_maximum_fusion.1, ...), channel_id=1, replica_groups=mesh['dp'=4,'sp'=16] {'sp'}, use_global_device_ids=true, to_apply=%region_27.28 | all-reduce | flops 2048 | bytes 16384 | tf_op jit(solution)/shard_map/pmax | solution.py:72
  112.5 0.4 fusion.99
  113.4 2.0 scatter_fusion.1
  115.4 4.2 %fusion.39 = f32[16,8,4,128]{3,2,1,0:T(4,128)} fusion(bf16[16,128,8,128]{3,2,1,0:T(8,128)(2,1)} %scatter_fusion.1, f32[16,8,4,128]{3,2,1,0:T(4,128)S(1)} %get-tuple-element.62, f32[16,8,4]{2,1,0:T(8,128)S(1)} %get-tuple-element.16, f32[16,8,4]{2,1,0:T(8,128)S(1)} %broadcast_maximum_fusion.3), kind=kOutput, calls=%fused_computation.37 | convolution fusion | flops 16973824 | bytes 4722688 | tf_op jit(solution)/shard_map/bkgs,bskd->bkgd/dot_general | solution.py:52
  119.6 2.0 scatter_fusion.3
  121.6 4.2 %fusion.45 = f32[16,8,4,128]{3,2,1,0:T(4,128)} fusion(bf16[16,128,8,128]{3,2,1,0:T(8,128)(2,1)} %scatter_fusion.3, f32[16,8,4,128]{3,2,1,0:T(4,128)S(1)} %get-tuple-element.60, f32[16,8,4]{2,1,0:T(8,128)S(1)} %get-tuple-element.64, f32[16,8,4]{2,1,0:T(8,128)S(1)} %broadcast_maximum_fusion.2), kind=kOutput, calls=%fused_computation.39 | convolution fusion | flops 16973824 | bytes 4722688 | tf_op jit(solution)/shard_map/bkgs,bskd->bkgd/dot_general | solution.py:52
  125.7 2.0 scatter_fusion.5
  127.8 4.2 %fusion.51 = f32[16,8,4,128]{3,2,1,0:T(4,128)} fusion(bf16[16,128,8,128]{3,2,1,0:T(8,128)(2,1)} %scatter_fusion.5, f32[16,8,4,128]{3,2,1,0:T(4,128)S(1)} %get-tuple-element.58, f32[16,8,4]{2,1,0:T(8,128)S(1)} %get-tuple-element.20, f32[16,8,4]{2,1,0:T(8,128)S(1)} %broadcast_maximum_fusion.1), kind=kOutput, calls=%fused_computation.41 | convolution fusion | flops 16973824 | bytes 4722688 | tf_op jit(solution)/shard_map/bkgs,bskd->bkgd/dot_general | solution.py:52
  131.9 2.0 scatter_fusion.7
  133.9 4.2 %fusion.57 = f32[16,8,4,128]{3,2,1,0:T(4,128)} fusion(bf16[16,128,8,128]{3,2,1,0:T(8,128)(2,1)} %scatter_fusion.7, f32[16,8,4,128]{3,2,1,0:T(4,128)S(1)} %get-tuple-element.56, f32[16,8,4]{2,1,0:T(8,128)S(1)} %get-tuple-element.66, f32[16,8,4]{2,1,0:T(8,128)S(1)} %broadcast_maximum_fusion), kind=kOutput, calls=%fused_computation.43 | convolution fusion | flops 16973824 | bytes 4722688 | tf_op jit(solution)/shard_map/bkgs,bskd->bkgd/dot_general | solution.py:52
  138.2 50.2 %all-reduce = (f32[16,8,4]{2,1,0:T(8,128)S(1)}, f32[16,8,4]{2,1,0:T(8,128)S(1)}, f32[16,8,4]{2,1,0:T(8,128)S(1)}, f32[16,8,4]{2,1,0:T(8,128)S(1)}) all-reduce(f32[16,8,4]{2,1,0:T(8,128)S(1)} %get-tuple-element.65, f32[16,8,4]{2,1,0:T(8,128)S(1)} %get-tuple-element.19, ...), channel_id=1, replica_groups=mesh['dp'=4,'sp'=16] {'sp'}, use_global_device_ids=true, to_apply=%region_30.31 | all-reduce | flops 2048 | bytes 16384 | tf_op jit(solution)/shard_map/psum | solution.py:74
  188.4 57.4 %all-reduce.5.cloned.1.call-done = (f32[16,8,4,128]{3,2,1,0:T(4,128)}, f32[16,8,4,128]{3,2,1,0:T(4,128)}, f32[16,8,4,128]{3,2,1,0:T(4,128)}, f32[16,8,4,128]{3,2,1,0:T(4,128)}) async-done(((f32[16,8,4,128]{3,2,1,0:T(4,128)}, f32[16,8,4,128]{3,2,1,0:T(4,128)}, f32[16,8,4,128]{3,2,1,0:T(4,128)}, f32[16,8,4,128]{3,2,1,0:T(4,128)}), (f32[16,8,4,128]{3,2,1,0:T(4,128)}, f32[16,8,4,128]{3,2,1,0:T(4,128)}, ...) | async-done | bytes 1048592 | tf_op jit(solution)/shard_map/psum | solution.py:74
  245.8 1.2 divide_convert_fusion
  247.0 1.2 divide_convert_fusion.1
  248.2 1.2 divide_convert_fusion.2
  249.5 1.2 divide_convert_fusion.3
  250.7 11.4 %fusion.33 = bf16[4,16,2560]{2,1,0:T(8,128)(2,1)} fusion(bf16[4096,2560]{1,0:T(8,128)(2,1)} %param.19, bf16[4,16,2560]{2,1,0:T(8,128)(2,1)S(1)} %copy-done, bf16[1,16,4096]{2,1,0:T(8,128)(2,1)S(1)} %stack_reshape.15, bf16[1,16,4096]{2,1,0:T(8,128)(2,1)S(1)} %stack_reshape.14, bf16[1,16,4096]{2,1,0:T(8,128)(2,1)S(1)} %stack_reshape.13, ...), kind=kOutput, calls=%fused_computation.35 | convolution fusion | flops 1343455232 | bytes 22151168 | tf_op jit(solution)/shard_map/dot_general | solution.py:77
  (59 shorter events, 3.7 us)
Async XLA Ops:
  7.2 238.6 %all-reduce.5.cloned.1.call-start = ((), (), s32[]{:S(2)}) async-start(), calls=%async_computation | async-start | bytes 2097152 | tf_op jit(solution)/shard_map/psum | solution.py:74
  7.2 4.8 %copy-start.1 = (bf16[16,128,8,128]{3,2,1,0:T(8,128)(2,1)S(1)}, bf16[16,128,8,128]{3,2,1,0:T(8,128)(2,1)}, u32[]{:S(2)}) copy-start(bf16[16,128,8,128]{3,2,1,0:T(8,128)(2,1)} %param.12) | copy-start | bytes 12582916
  12.0 2.0 copy-start.3
  12.0 2.1 copy-start.2
  12.0 2.1 copy-start
  14.0 4.0 %copy-start.4 = (bf16[128]{0:T(256)(128)(2,1)S(1)}, bf16[128]{0:T(256)(128)(2,1)}, u32[]{:S(2)}) copy-start(bf16[128]{0:T(256)(128)(2,1)} %param.20) | copy-start | bytes 772
  14.3 13.5 %slice-start = ((s8[5242880]{0:T(1024)(128)(4,1)}), s8[4194304]{0:T(1024)(128)(4,1)S(1)}, s32[]{:S(2)}) async-start(s8[5242880]{0:T(1024)(128)(4,1)} %bitcast.116), calls=%async_computation.1 | async-start | bytes 8388608
  18.1 9.7 %copy-start.5 = (bf16[128]{0:T(256)(128)(2,1)S(1)}, bf16[128]{0:T(256)(128)(2,1)}, u32[]{:S(2)}) copy-start(bf16[128]{0:T(256)(128)(2,1)} %param.21) | copy-start | bytes 772
  18.1 9.7 %slice-start.1 = ((s8[5242880]{0:T(1024)(128)(4,1)}), s8[1048576]{0:T(1024)(128)(4,1)S(1)}, s32[]{:S(2)}) async-start(s8[5242880]{0:T(1024)(128)(4,1)} %bitcast.116), calls=%async_computation.2 | async-start | bytes 2097152
Sparse Core Ops, SparseCore 0:
  138.3 107.4 all-reduce.4
where the time goes:
time: 270 us; the launch traced here: 269 us
  blocking collectives  104 us (39%)
  matrix products  60 us (22%)
  waiting for transfers between devices  57.4 us (21%)
  local copies, waits for them, and re-layouts  23.6 us (9%)
  between operations  14.6 us (5%)
  other arithmetic  8.87 us (3%)
    psum x1, waiting for transfers between devices, per_device(): lax.psum((part_out * factor[..., None], row_sum * factor), 'sp')  57.4 us
    pmax x1, blocking collectives, per_device(): glob_max = lax.pmax(row_max, 'sp')  54.2 us
    psum x1, blocking collectives, per_device(): lax.psum((part_out * factor[..., None], row_sum * factor), 'sp')  50.2 us
    dot_general x4, matrix products, local_partial(): jnp.einsum('bkgd,bskd->bkgs', grouped, k_local, preferred_element_type=jn...  18.1 us
    dot_general x4, matrix products, local_partial(): jnp.einsum('bkgs,bskd->bkgd', weights.astype(jnp.bfloat16), v_local, pref...  16.6 us
    dot_general x3, matrix products, heads_of(): jnp.dot(normed, weight, preferred_element_type=jnp.float32)  13.9 us
    dot_general x1, matrix products, per_device(): out_proj = jnp.dot(attended, w_o, preferred_element_type=jnp.float32)  11.4 us
    scatter x4, local copies, waits for them, and re-layouts, per_device(): k_local = k_local.at[rows, write_pos].set(keys_new[step], mode='drop')  8.21 us
  transfers between devices with their start and end apart: 1, of which 1 were waited for; matrix products, arithmetic and copies ran while one was open for 0% of the time, Pallas kernels for 0%

commit v1 on v0

v1 whole, which is shorter than its diff:
```python
import functools
import math
import jax
import jax.numpy as jnp
from jax import lax
from jax.experimental import pallas as pl
from jax.experimental.pallas import tpu as pltpu
from jax.sharding import PartitionSpec as P

NORM_EPS = 1e-6
ROPE_BASE = 1000000.0
MESH = pl.DeviceIdType.MESH
NEG = -1e30
COLS = 512
ROWS = 16
MSG = 8
VMEM_LIMIT = 67043328


def attend_kernel(dims, lens, x_ref, gain_ref, qg_ref, kg_ref, wq_hbm, wk_hbm, wv_hbm, kc_hbm, vc_hbm,
                  part_ref, ko_hbm, vo_hbm,
                  wbuf, kbuf, vbuf, h_ref, cos_ref, sin_ref, q_rows, k_rows, v_rows, colid, s_buf, p_buf,
                  w_sem, k_sem, v_sem, ko_sem, vo_sem):
    steps, batch, slots, kv_heads, head_dim, q_heads = dims
    group = q_heads // kv_heads
    half_heads = q_heads // 2
    rows = steps * batch
    kv_cols = kv_heads * head_dim // COLS
    q_cols = q_heads * head_dim // COLS
    per_chunk = COLS // head_dim
    first_slot = lax.axis_index('sp') * slots

    def weight_copy(index, source, column):
        return pltpu.make_async_copy(source.at[:, pl.ds(column * COLS, COLS)], wbuf.at[index], w_sem.at[index])

    def cache_copy(b, source, target, sems):
        return pltpu.make_async_copy(source.at[b], target.at[b], sems.at[b])

    for i in range(kv_cols):
        weight_copy(i, wk_hbm, i).start()
    for i in range(kv_cols):
        weight_copy(kv_cols + i, wv_hbm, i).start()
    for b in range(batch):
        cache_copy(b, kc_hbm, kbuf, k_sem).start()
        cache_copy(b, vc_hbm, vbuf, v_sem).start()
    for i in range(q_cols):
        weight_copy(2 * kv_cols + i, wq_hbm, i).start()

    x = x_ref[...].astype(jnp.float32)
    inv = lax.rsqrt(jnp.mean(x * x, axis=-1, keepdims=True) + NORM_EPS)
    h_ref[...] = (x * inv * gain_ref[...].astype(jnp.float32)).astype(jnp.bfloat16)

    row = lax.broadcasted_iota(jnp.int32, (rows, head_dim), 0)
    lane = lax.broadcasted_iota(jnp.int32, (rows, head_dim), 1)
    position = row // batch
    for b in range(batch):
        position = position + jnp.where(row % batch == b, lens[b], 0)
    half_dim = head_dim // 2
    freq = jnp.exp((lane % half_dim).astype(jnp.float32) * (-2.0 * math.log(ROPE_BASE) / head_dim))
    angle = position.astype(jnp.float32) * freq
    cos_ref[...] = jnp.cos(angle)
    sine = jnp.sin(angle)
    sin_ref[...] = jnp.where(lane < half_dim, -sine, sine)

    col = lax.broadcasted_iota(jnp.int32, (ROWS, slots * kv_heads), 1)
    head = lax.broadcasted_iota(jnp.int32, (ROWS, slots * kv_heads), 0)
    for half in range(2):
        match = (half * half_heads + head) // group == col % kv_heads
        colid[half] = jnp.where(match, col, jnp.int32(2 ** 30))

    def head_norm(values, gain):
        inv = lax.rsqrt(jnp.mean(values * values, axis=-1, keepdims=True) + NORM_EPS)
        values = values * inv * gain
        return values * cos_ref[...] + pltpu.roll(values, half_dim, 1) * sin_ref[...]

    def project(index):
        out = jnp.dot(h_ref[...], wbuf[index], preferred_element_type=jnp.float32)
        return out.astype(jnp.bfloat16).astype(jnp.float32)

    kg = kg_ref[...].astype(jnp.float32)
    qg = qg_ref[...].astype(jnp.float32)
    for i in range(kv_cols):
        weight_copy(i, wk_hbm, i).wait()
        out = project(i)
        for n in range(per_chunk):
            k_rows[pl.ds(i * per_chunk + n, rows, stride=kv_heads), :] = head_norm(out[:, n * head_dim:(n + 1) * head_dim], kg)
    for i in range(kv_cols):
        weight_copy(kv_cols + i, wv_hbm, i).wait()
        out = project(kv_cols + i)
        for n in range(per_chunk):
            v_rows[pl.ds(i * per_chunk + n, rows, stride=kv_heads), :] = out[:, n * head_dim:(n + 1) * head_dim]

    def update(b, _):
        cache_copy(b, kc_hbm, kbuf, k_sem).wait()
        cache_copy(b, vc_hbm, vbuf, v_sem).wait()
        for t in range(steps):
            slot = lens[b] + t - first_slot

            @pl.when((slot >= 0) & (slot < slots))
            def _():
                start = pl.multiple_of(slot // 2 * 2 * kv_heads, 2 * kv_heads)
                upper = lax.broadcasted_iota(jnp.int32, (2 * kv_heads, head_dim), 0) // kv_heads
                for buf, new in ((kbuf, k_rows), (vbuf, v_rows)):
                    fresh = new[pl.ds(pl.multiple_of((t * batch + b) * kv_heads, kv_heads), kv_heads), :]
                    fresh = jnp.concatenate([fresh, fresh], axis=0)
                    old = buf[b, pl.ds(start, 2 * kv_heads), :].astype(jnp.float32)
                    buf[b, pl.ds(start, 2 * kv_heads), :] = jnp.where(upper == slot % 2, fresh, old).astype(jnp.bfloat16)
        return 0

    lax.fori_loop(0, batch, update, 0)

    def project_q(i, _):
        weight_copy(2 * kv_cols + i, wq_hbm, i).wait()
        out = project(2 * kv_cols + i)
        for n in range(per_chunk):
            q_rows[pl.ds(i * per_chunk + n, rows, stride=q_heads), :] = head_norm(out[:, n * head_dim:(n + 1) * head_dim], qg)
        return 0

    lax.fori_loop(0, q_cols, project_q, 0)

    def write_back(b, _):
        cache_copy(b, kbuf, ko_hbm, ko_sem).start()
        cache_copy(b, vbuf, vo_hbm, vo_sem).start()
        return 0

    lax.fori_loop(0, batch, write_back, 0)

    scale = head_dim ** -0.5 * math.log2(math.e)

    def scores(b, place):
        q = []
        for half in range(2):
            for t in range(steps):
                start = pl.multiple_of((t * batch + b) * q_heads + half * half_heads, half_heads)
                q.append(q_rows[pl.ds(start, half_heads), :].astype(jnp.bfloat16))
        q = jnp.concatenate(q, axis=0)
        s_buf[place] = lax.dot_general(q, kbuf[b], (((1,), (1,)), ((), ())), preferred_element_type=jnp.float32)

    def soften(b, place):
        diag_lane = lax.broadcasted_iota(jnp.int32, (ROWS, head_dim), 1)
        diag_row = lax.broadcasted_iota(jnp.int32, (ROWS, head_dim), 0)
        sub = lax.broadcasted_iota(jnp.int32, (MSG, head_dim), 0)
        for half in range(2):
            max_sum = jnp.zeros((ROWS, head_dim), jnp.float32)
            den_sum = jnp.zeros((ROWS, head_dim), jnp.float32)
            for t in range(steps):
                r0 = (half * steps + t) * ROWS
                limit = (lens[b] + t - first_slot + 1) * kv_heads
                s = jnp.where(colid[half] < limit, s_buf[place, r0:r0 + ROWS, :] * scale, -jnp.inf)
                top = jnp.maximum(jnp.max(s, axis=-1, keepdims=True), NEG)
                p = jnp.exp2(s - top)
                den = jnp.sum(p, axis=-1, keepdims=True)
                p_buf[place, r0:r0 + ROWS, :] = p.astype(jnp.bfloat16)
                own = diag_lane == diag_row + t * ROWS
                max_sum = max_sum + jnp.where(own, top, 0.0)
                den_sum = den_sum + jnp.where(own, den, 0.0)
            max_row = jnp.sum(max_sum, axis=0, keepdims=True)
            den_row = jnp.sum(den_sum, axis=0, keepdims=True)
            stats = jnp.where(sub == 0, max_row, jnp.where(sub == 1, den_row, 0.0))
            part_ref[half, b, steps * half_heads:, :] = stats

    def mix(b, place):
        out = jnp.dot(p_buf[place], vbuf[b], preferred_element_type=jnp.float32)
        for half in range(2):
            part_ref[half, b, :steps * half_heads, :] = out[half * steps * half_heads:(half + 1) * steps * half_heads]

    def attend(i, _):
        for place in range(2):
            scores(2 * i + place, place)
        for place in range(2):
            soften(2 * i + place, place)
        for place in range(2):
            mix(2 * i + place, place)
        return 0

    lax.fori_loop(0, batch // 2, attend, 0)

    def finish(b, _):
        cache_copy(b, kbuf, ko_hbm, ko_sem).wait()
        cache_copy(b, vbuf, vo_hbm, vo_sem).wait()
        return 0

    lax.fori_loop(0, batch, finish, 0)


def combine_kernel(dims, part_ref, x_ref, wo_hbm, y_ref,
                   wbuf, pair_in, own, out_s4, out_3, in_s4, in_3, in_f1, in_f2, fin, half_in, half_out,
                   mine, other,
                   w_sem, pair_send, pair_recv, rs_send, rs_recv, half_sem, ag_send, ag_recv, d2d_send, d2d_recv):
    steps, batch, q_heads, head_dim, hidden, chips = dims
    half_heads = q_heads // 2
    per_chip = batch // chips
    body = steps * half_heads
    msg = body + MSG
    half_cols = hidden // 2
    tiles = half_cols // head_dim
    block = per_chip * steps
    sp = lax.axis_index('sp')
    chip, core = sp // 2, sp % 2

    def chip_at(offset):
        return lax.rem(chip + offset + chips, chips)

    def device(offset):
        return {'sp': chip_at(offset) * 2 + core}

    partner = {'sp': chip * 2 + 1 - core}

    depth = q_heads * head_dim // 2
    parts = 4
    piece = depth // parts

    def weight_copy(i):
        start = pl.multiple_of(core * depth + i * piece, piece)
        return pltpu.make_async_copy(wo_hbm.at[pl.ds(start, piece), :], wbuf.at[i], w_sem.at[i])

    for i in range(parts):
        weight_copy(i).start()

    barrier = pltpu.get_barrier_semaphore()
    pl.semaphore_signal(barrier, inc=1, device_id=partner, device_id_type=MESH)
    for offset in (1, -1, 2, -2):
        pl.semaphore_signal(barrier, inc=1, device_id=device(offset), device_id_type=MESH)
    pl.semaphore_wait(barrier, 5)

    order = (4, 3, -3, 1, -1, 2, -2, 0)

    def pair_copy(i):
        start = pl.multiple_of(chip_at(order[i]) * per_chip, per_chip)
        return pltpu.make_async_remote_copy(
            src_ref=part_ref.at[1 - core, pl.ds(start, per_chip)], dst_ref=pair_in.at[i],
            send_sem=pair_send.at[i], recv_sem=pair_recv.at[i], device_id=partner, device_id_type=MESH)

    for i in range(len(order)):
        pair_copy(i).start()

    lane = lax.broadcasted_iota(jnp.int32, (body, head_dim), 1)
    row = lax.broadcasted_iota(jnp.int32, (body, head_dim), 0)
    diag = lane == row
    sub = lax.broadcasted_iota(jnp.int32, (MSG, head_dim), 0)

    def column(values):
        return jnp.sum(jnp.where(diag, values, 0.0), axis=-1, keepdims=True)

    def merge(pieces, last=False):
        tops = [p[body:body + 1, :] for p in pieces]
        dens = [p[body + 1:body + 2, :] for p in pieces]
        top = functools.reduce(jnp.maximum, tops)
        factors = [jnp.exp2(t - top) for t in tops]
        den = sum(f * d for f, d in zip(factors, dens))
        if last:
            factors = [f / den for f in factors]
        out = sum(column(f) * p[:body, :] for f, p in zip(factors, pieces))
        return out, jnp.where(sub == 0, top, jnp.where(sub == 1, den, 0.0))

    def reduce_into(target, pieces):
        out, stats = merge(pieces)
        target[:body, :] = out
        target[body:, :] = stats

    def mine_of(i, j):
        return part_ref.at[core, chip_at(order[i]) * per_chip + j]

    sends = []

    def send(src, dst, index, offset):
        copy = pltpu.make_async_remote_copy(
            src_ref=src, dst_ref=dst, send_sem=rs_send.at[index], recv_sem=rs_recv.at[index],
            device_id=device(offset), device_id_type=MESH)
        copy.start()
        sends.append(copy)
        return copy

    def pair_merge(i, target):
        pair_copy(i).wait_recv()
        for j in range(per_chip):
            reduce_into(target.at[j], [mine_of(i, j), pair_in.at[i, j]])

    pair_merge(0, out_s4)
    far = [send(out_s4.at[j], in_s4.at[j], j, 2 if j == 0 else -2) for j in range(per_chip)]
    third = []
    for d, sign in enumerate((1, -1)):
        pair_merge(1 + d, out_3.at[d])
        third.append([send(out_3.at[d, j], in_3.at[d, j], 2 + 2 * d + j, sign) for j in range(per_chip)])
    first = []
    for d, sign in enumerate((1, -1)):
        pair_merge(3 + d, own.at[d])
        first.append([send(own.at[d, j], in_f1.at[d, j], 6 + 2 * d + j, sign) for j in range(per_chip)])
    second = []
    for d, sign in enumerate((1, -1)):
        pair_copy(5 + d).wait_recv()
        second.append([])
    for j in range(per_chip):
        for d, sign in enumerate((1, -1)):
            pieces = [mine_of(5 + d, j), pair_in.at[5 + d, j]]
            third[d][j].wait_recv()
            pieces.append(in_3.at[d, j])
            if j == d:
                far[j].wait_recv()
                pieces.append(in_s4.at[j])
            reduce_into(own.at[2 + d, j], pieces)
            second[d].append(send(own.at[2 + d, j], in_f2.at[d, j], 10 + 2 * d + j, 2 * sign))
    pair_copy(7).wait_recv()
    for j in range(per_chip):
        pieces = [mine_of(7, j), pair_in.at[7, j]]
        for d in range(2):
            first[d][j].wait_recv()
            pieces.append(in_f1.at[d, j])
        for d in range(2):
            second[d][j].wait_recv()
            pieces.append(in_f2.at[d, j])
        fin[j * body:(j + 1) * body, :] = merge(pieces, last=True)[0]

    o = jnp.concatenate([fin[pl.ds(n, block, stride=half_heads), :] for n in range(half_heads)], axis=1).astype(jnp.bfloat16)
    acc = None
    for i in range(parts):
        weight_copy(i).wait()
        term = jnp.dot(o[:, i * piece:(i + 1) * piece], wbuf[i], preferred_element_type=jnp.float32)
        acc = term if acc is None else acc + term

    for n in range(tiles):
        left = acc[:, n * head_dim:(n + 1) * head_dim]
        right = acc[:, half_cols + n * head_dim:half_cols + (n + 1) * head_dim]
        half_out[0, n] = jnp.where(core == 0, right, left)
        half_out[1, n] = jnp.where(core == 0, left, right)
    swap = pltpu.make_async_remote_copy(
        src_ref=half_out.at[0], dst_ref=half_in, send_sem=half_sem.at[0], recv_sem=half_sem.at[1],
        device_id=partner, device_id_type=MESH)
    swap.start()
    swap.wait_recv()

    def rows_of(offset):
        return pl.ds(pl.multiple_of(chip_at(offset) * block, block), block)

    for n in range(tiles):
        mine[n, rows_of(0), :] = (x_ref[core, n, rows_of(0), :] + half_out[1, n] + half_in[n]).astype(jnp.bfloat16).astype(jnp.float32)

    gathers = []

    def gather(offset, target, index, span=(0, tiles)):
        view = mine.at[span[0]:span[1], rows_of(offset), :]
        copy = pltpu.make_async_remote_copy(
            src_ref=view, dst_ref=view, send_sem=ag_send.at[index], recv_sem=ag_recv.at[index],
            device_id=device(target), device_id_type=MESH)
        copy.start()
        gathers.append(copy)
        return copy

    def forward(offset, index, span=(0, tiles)):
        copy = pltpu.make_async_remote_copy(
            src_ref=mine.at[span[0]:span[1], rows_of(offset), :], dst_ref=other.at[span[0]:span[1], rows_of(offset), :],
            send_sem=d2d_send.at[index], recv_sem=d2d_recv.at[index], device_id=partner, device_id_type=MESH)
        copy.start()
        return copy

    mid = tiles // 2
    spans = ((0, mid), (mid, tiles))
    direct2 = [gather(0, 2 * sign, d) for d, sign in enumerate((1, -1))]
    direct1 = [gather(0, sign, 2 + d) for d, sign in enumerate((1, -1))]
    moved = [forward(0, 0)]
    relay4, relay3 = [], []
    for d, sign in enumerate((1, -1)):
        direct2[d].wait_recv()
        relay4.append(gather(-2 * sign, 2 * sign, 4 + d, spans[d]))
        relay3.append(gather(-2 * sign, sign, 6 + d))
        moved.append(forward(-2 * sign, 1 + d))
    for d, sign in enumerate((1, -1)):
        direct1[d].wait_recv()
        moved.append(forward(-sign, 3 + d))
    for d, sign in enumerate((1, -1)):
        relay3[d].wait_recv()
        moved.append(forward(-3 * sign, 5 + d))
    for d, sign in enumerate((1, -1)):
        relay4[d].wait_recv()
        moved.append(forward(-4 * sign, 7 + d, spans[d]))
    for copy in moved:
        copy.wait_recv()

    for n in range(tiles):
        for t in range(steps):
            here = mine[n, pl.ds(t, batch, stride=steps), :]
            there = other[n, pl.ds(t, batch, stride=steps), :]
            y_ref[t, :, n * head_dim:(n + 1) * head_dim] = jnp.where(core == 0, here, there).astype(jnp.bfloat16)
            y_ref[t, :, half_cols + n * head_dim:half_cols + (n + 1) * head_dim] = jnp.where(core == 0, there, here).astype(jnp.bfloat16)

    for i in range(len(order)):
        pair_copy(i).wait_send()
    for copy in sends + [swap] + gathers + moved:
        copy.wait_send()


def solution(mesh):
    chips = mesh.shape['sp'] // 2
    assert chips == 8

    def per_device(x_steps, k_local, v_local, seq_lens, norm_gain, w_q, w_k, w_v, w_o, q_gain, k_gain):
        steps, batch, hidden = x_steps.shape
        slots, kv_heads, head_dim = k_local.shape[1:]
        q_heads = w_q.shape[1] // head_dim
        half_heads = q_heads // 2
        rows = steps * batch
        msg = steps * half_heads + MSG
        assert half_heads == ROWS and batch == 2 * chips
        vmem = pl.BlockSpec(memory_space=pltpu.VMEM)
        hbm = pl.BlockSpec(memory_space=pltpu.HBM)
        smem = pl.BlockSpec(memory_space=pltpu.SMEM)
        chunks = (w_q.shape[1] + w_k.shape[1] + w_v.shape[1]) // COLS
        flat = (batch, slots * kv_heads, head_dim)
        bf16, f32 = jnp.bfloat16, jnp.float32
        part, k_new, v_new = pl.pallas_call(
            functools.partial(attend_kernel, (steps, batch, slots, kv_heads, head_dim, q_heads)),
            out_shape=(jax.ShapeDtypeStruct((2, batch, msg, head_dim), f32), jax.ShapeDtypeStruct(flat, bf16), jax.ShapeDtypeStruct(flat, bf16)),
            in_specs=[smem, vmem, vmem, vmem, vmem, hbm, hbm, hbm, hbm, hbm],
            out_specs=(vmem, hbm, hbm),
            scratch_shapes=[
                pltpu.VMEM((chunks, hidden, COLS), bf16), pltpu.VMEM(flat, bf16), pltpu.VMEM(flat, bf16),
                pltpu.VMEM((rows, hidden), bf16), pltpu.VMEM((rows, head_dim), f32), pltpu.VMEM((rows, head_dim), f32),
                pltpu.VMEM((rows * q_heads, head_dim), f32), pltpu.VMEM((rows * kv_heads, head_dim), f32),
                pltpu.VMEM((rows * kv_heads, head_dim), f32), pltpu.VMEM((2, ROWS, slots * kv_heads), jnp.int32),
                pltpu.VMEM((2, steps * q_heads, slots * kv_heads), f32), pltpu.VMEM((2, steps * q_heads, slots * kv_heads), bf16),
                pltpu.SemaphoreType.DMA((chunks,)), pltpu.SemaphoreType.DMA((batch,)), pltpu.SemaphoreType.DMA((batch,)),
                pltpu.SemaphoreType.DMA((batch,)), pltpu.SemaphoreType.DMA((batch,)),
            ],
            compiler_params=pltpu.CompilerParams(vmem_limit_bytes=VMEM_LIMIT),
            name='attend',
        )(seq_lens, x_steps.reshape(rows, hidden), norm_gain.reshape(1, -1), q_gain.reshape(1, -1), k_gain.reshape(1, -1),
          w_q, w_k, w_v, k_local.reshape(flat), v_local.reshape(flat))

        tiles = hidden // 2 // head_dim
        block = batch // chips * steps
        x_tiles = x_steps.astype(f32).reshape(steps, batch, 2, tiles, head_dim).transpose(2, 3, 1, 0, 4).reshape(2, tiles, rows, head_dim)
        pair = (batch // chips, msg, head_dim)
        sem = pltpu.SemaphoreType.DMA
        y_steps = pl.pallas_call(
            functools.partial(combine_kernel, (steps, batch, q_heads, head_dim, hidden, chips)),
            out_shape=jax.ShapeDtypeStruct(x_steps.shape, bf16),
            in_specs=[vmem, vmem, hbm],
            out_specs=vmem,
            scratch_shapes=[
                pltpu.VMEM((4, q_heads * head_dim // 8, hidden), bf16), pltpu.VMEM((8,) + pair, f32), pltpu.VMEM((4,) + pair, f32),
                pltpu.VMEM(pair, f32), pltpu.VMEM((2,) + pair, f32), pltpu.VMEM(pair, f32), pltpu.VMEM((2,) + pair, f32),
                pltpu.VMEM((2,) + pair, f32), pltpu.VMEM((2,) + pair, f32),
                pltpu.VMEM((batch // chips * steps * half_heads, head_dim), f32),
                pltpu.VMEM((tiles, block, head_dim), f32), pltpu.VMEM((2, tiles, block, head_dim), f32),
                pltpu.VMEM((tiles, rows, head_dim), f32), pltpu.VMEM((tiles, rows, head_dim), f32),
                sem((4,)), sem((8,)), sem((8,)), sem((14,)), sem((14,)), sem((2,)), sem((8,)), sem((8,)), sem((9,)), sem((9,)),
            ],
            compiler_params=pltpu.CompilerParams(vmem_limit_bytes=VMEM_LIMIT, collective_id=0, has_side_effects=True),
            name='combine',
        )(part, x_tiles, w_o)
        return y_steps, k_new.reshape(k_local.shape), v_new.reshape(v_local.shape)

    cache_spec = P('dp', 'sp', None, None)
    step_spec = P(None, 'dp', None)
    return jax.shard_map(per_device, mesh=mesh, in_specs=(step_spec, cache_spec, cache_spec, P('dp'), P(), P(), P(), P(), P(), P(), P()), out_specs=(step_spec, cache_spec, cache_spec), check_vma=False)
```

time: 270 us -> 68.1 us (0.25)
  blocking collectives: 104 us -> 0 us
  Pallas kernels: 0 us -> 61.7 us
  matrix products: 60 us -> 0 us
  waiting for transfers between devices: 57.4 us -> 0 us
  local copies, waits for them, and re-layouts: 23.6 us -> 5.46 us
  between operations: 14.6 us -> 0.65 us
  other arithmetic: 8.87 us -> 0 us
    pallas_call x0 -> x2, Pallas kernels: none -> 61.7 us  [the longest x1 35.6 us: per_device(): pl.pallas_call(functools.partial(combine_kernel, (steps, batch, q_heads,...]
    dot_general x12 -> x0, matrix products: 60 us -> none  [the longest x4 18.1 us: local_partial(): jnp.einsum('bkgd,bskd->bkgs', grouped, k_local, preferred_element_type=jn...]
    psum x1 -> x0, waiting for transfers between devices: 57.4 us -> none  [per_device(): lax.psum((part_out * factor[..., None], row_sum * factor), 'sp')]
    pmax x1 -> x0, blocking collectives: 54.2 us -> none  [per_device(): glob_max = lax.pmax(row_max, 'sp')]
    psum x1 -> x0, blocking collectives: 50.2 us -> none  [per_device(): lax.psum((part_out * factor[..., None], row_sum * factor), 'sp')]
    scatter x8 -> x0, local copies, waits for them, and re-layouts: 16.2 us -> none  [the longest x4 8.21 us: per_device(): k_local = k_local.at[rows, write_pos].set(keys_new[step], mode='drop')]
    unnamed x25 -> x1, local copies, waits for them, and re-layouts: 7.09 us -> 1.72 us
    convert_element_type x8 -> x0, other arithmetic: 4.64 us -> none  [the longest x4 4.62 us: per_device(): (numerator / denominator[..., None]).astype(jnp.bfloat16).reshape(batch, -1)]
  transfers between devices with their start and end apart: 1 -> 0, of which waited for: 1 -> 0; matrix products, arithmetic and copies ran while one was open for 0% -> 0% of each run, Pallas kernels for 0% -> 0%
where the time goes in v1:
time: 68.1 us; the launch traced here: 67.8 us
  Pallas kernels  61.7 us (91%)
  local copies, waits for them, and re-layouts  5.46 us (8%)
    pallas_call x1, Pallas kernels, per_device(): pl.pallas_call(functools.partial(combine_kernel, (steps, batch, q_heads,...  35.6 us
    pallas_call x1, Pallas kernels, per_device(): pl.pallas_call(functools.partial(attend_kernel, (steps, batch, slots, kv_...  26 us
    reshape x2, local copies, waits for them, and re-layouts, per_device(): x_steps.astype(f32).reshape(steps, batch, 2, tiles, head_dim)  2.44 us
    unnamed x1, local copies, waits for them, and re-layouts  1.72 us

profile of v1, /device:TPU:21, one launch (start us, length us, event | category | flops | bytes accessed | tf_op | source)
XLA Modules:
  0.0 67.8 jit_solution(6068162582006188580)
XLA Ops:
  0.6 1.3 %reshape.40.gain_ref = bf16[1,2560]{1,0:T(2,128)(2,1)} reshape(bf16[2560]{0:T(1024)(128)(2,1)} %param.15) | data formatting | bytes 10240 | tf_op jit(solution)/shard_map/reshape | solution.py:426
  1.9 1.1 %reshape.54 = f32[4,16,2,10,128]{4,3,2,1,0:T(8,128)S(1)} reshape(bf16[4,16,2560]{2,1,0:T(8,128)(2,1)} %param.11) | data formatting | bytes 983040 | tf_op jit(solution)/shard_map/reshape | solution.py:431
  3.1 1.3 %copy.15 = f32[2,10,16,4,128]{4,3,2,1,0:T(4,128)} copy(f32[2,10,16,4,128]{4,1,0,2,3:T(8,128)S(1)} %bitcast.9) | data formatting | bytes 1310720 | tf_op jit(solution)/shard_map/reshape | solution.py:431
  4.4 26.0 %attend.1 = (f32[2,16,72,128]{3,2,1,0:T(8,128)}, bf16[16,1024,128]{2,1,0:T(8,128)(2,1)}, bf16[16,1024,128]{2,1,0:T(8,128)(2,1)}) custom-call(s32[16]{0:T(128)} %lens.1, bf16[64,2560]{1,0:T(8,128)(2,1)} %bitcast.13, bf16[1,2560]{1,0:T(2,128)(2,1)} %reshape.40.gain_ref, bf16[1,128]{1,0:T(2,128)(2,1)} %bitcast.14, bf16[1,128]{1,0:T(2,128)(2,1)} %bitcast.15, ...), custom_call_target="tpu_custom_call" | custom-call | tf_op jit(solution)/shard_map/attend/pallas_call | solution.py:410
  30.4 35.6 %combine.1 = bf16[4,16,2560]{2,1,0:T(8,128)(2,1)} custom-call(f32[2,16,72,128]{3,2,1,0:T(8,128)} %get-tuple-element.6.part_ref, f32[2,10,64,128]{3,2,1,0:T(8,128)} %bitcast.12, bf16[4096,2560]{1,0:T(8,128)(2,1)} %wo_hbm.1), custom_call_target="tpu_custom_call" | custom-call | tf_op jit(solution)/shard_map/combine/pallas_call | solution.py:434
  66.0 1.7 %copy.17 = bf16[4,16,2560]{2,1,0:T(8,128)(2,1)} copy(bf16[4,16,2560]{2,1,0:T(8,128)(2,1)} %combine.1) | data formatting | bytes 655360
